TPU v7x, 32 devices: a whole 2x2x4 slice. The times are simulated.
32 devices in a mesh: groups: 2 (over y), seq: 4 (over z), head: 2 (over x), inner: 2 (over core).
Axes of the slice: x: 2, y: 2, z: 4, core: 2. Of those that a mesh axis runs over, the one named last changes fastest.
Arguments:
- queries: bfloat16 [4096, 2, 8, 128], P(('groups', 'seq'), 'head', 'inner'), parts along dimension 0, may hold values from -120 to 120
- grad_out: bfloat16 [4096, 2, 8, 128], P(('groups', 'seq'), 'head', 'inner'), parts along dimension 0, may hold values from -6 to 6
- keys: bfloat16 [4096, 2, 128], P(('groups', 'seq'), 'head'), parts along dimension 0, may hold values from -6 to 6
- values: bfloat16 [4096, 2, 128], P(('groups', 'seq'), 'head'), parts along dimension 0, may hold values from -6 to 6
- indices: int32 [2, 64, 16], P('head', 'groups'), parts along dimension 1, may hold values from 0 to 31, as said below
- valid: int32 [2, 64, 16], P('head', 'groups'), parts along dimension 1, may hold values from 0 to 1
Outputs:
- grad_queries: bfloat16 [4096, 2, 8, 128], P(('groups', 'seq'), 'head', 'inner'), parts along dimension 0
- grad_keys: bfloat16 [4096, 2, 128], P(('groups', 'seq'), 'head'), parts along dimension 0
- grad_values: bfloat16 [4096, 2, 128], P(('groups', 'seq'), 'head'), parts along dimension 0
There are 2 independent parts, one for each index of `groups`. A program takes and returns all parts, laid end to end along the dimension named above; each array names one. Nothing has to cross between parts.
Inputs may be any that keep to these rules, and one draw needn't show every extreme that they name: `indices`: call blocks r * 8 to r * 8 + 7 run r. For every KV head and query block b: slot 0 names b and is valid; the valid slots name distinct blocks at most b; over all query blocks of run r, the valid slots name blocks of runs later than r never, and for each earlier run exactly 4 distinct blocks of it. Slots that are not valid name arbitrary blocks.
All inputs are finite; a program needn't handle non-finite values.
Results may differ from a plain program's by a relative error of at most 0.007.
Values may be sent and summed in bfloat16 or wider, within the bound.
No kernel may reach another device: no remote copies, remote signals or barrier semaphores. Data moves between devices by JAX's collectives and lax.ppermute only.
A program may use at most 64 MiB of HBM per device.

v0:
```python
import math

import jax
import jax.numpy as jnp
from jax import lax
from jax.sharding import PartitionSpec as P

BLK = 64
TOPK = 16
CAP = 4


def per_device(queries, grad_out, keys, values, indices, valid):
    tokens = queries.shape[0]
    heads_here = queries.shape[2]
    width = queries.shape[3]
    seq_count = lax.axis_size("seq")
    seq_here = lax.axis_index("seq")
    blocks_here = tokens // BLK
    total_blocks = indices.shape[1]
    scaling = 1.0 / math.sqrt(width)
    remote_rows = seq_count * CAP
    dest_rows = remote_rows + blocks_here
    picks_all = indices[0]
    valid_all = valid[0] > 0
    owner_all = picks_all // blocks_here
    local_all = picks_all % blocks_here
    my_picks = lax.dynamic_slice_in_dim(picks_all, seq_here * blocks_here, blocks_here, 0)
    my_valid = lax.dynamic_slice_in_dim(valid_all, seq_here * blocks_here, blocks_here, 0)
    my_owner = my_picks // blocks_here
    my_local = my_picks % blocks_here
    remote = my_valid & (my_owner != seq_here)
    block_ids = jnp.arange(total_blocks, dtype=jnp.int32)
    hits_in = (my_picks[:, :, None] == block_ids[None, None, :]) & remote[:, :, None]
    present_in = jnp.any(hits_in, axis=(0, 1)).reshape(seq_count, blocks_here)
    rank_in = jnp.cumsum(present_in.astype(jnp.int32), axis=1) - 1
    slot_ref = jnp.sum(jnp.where(hits_in, rank_in.reshape(-1)[None, None, :], 0), axis=2)
    row_index = jnp.where(remote, my_owner * CAP + slot_ref, remote_rows + my_local)
    source_run = block_ids // blocks_here
    incoming = valid_all & (owner_all == seq_here) & (source_run != seq_here)[:, None]
    hits_out = (
        local_all[:, :, None] == jnp.arange(blocks_here, dtype=jnp.int32)[None, None, :]
    ) & incoming[:, :, None]
    present_out = jnp.any(hits_out.reshape(seq_count, blocks_here * TOPK, blocks_here), axis=1)
    rank_out = jnp.cumsum(present_out.astype(jnp.int32), axis=1) - 1
    choose_out = present_out[:, None, :] & (
        rank_out[:, None, :] == jnp.arange(CAP, dtype=jnp.int32)[None, :, None]
    )
    wanted = my_picks.reshape(-1)
    blank = jnp.zeros((blocks_here * TOPK, BLK, width), jnp.bfloat16)
    carry = (blank, blank)
    key_piece = lax.all_gather(keys, "seq", axis=0, tiled=True)
    value_piece = lax.all_gather(values, "seq", axis=0, tiled=True)
    count = key_piece.shape[0] // BLK
    relative = wanted
    inside = (relative >= 0) & (relative < count)
    relative = jnp.clip(relative, 0, count - 1)
    key_rows = jnp.take(key_piece[:, 0].reshape(count, BLK, width), relative, axis=0)
    value_rows = jnp.take(value_piece[:, 0].reshape(count, BLK, width), relative, axis=0)
    sel_keys = jnp.where(inside[:, None, None], key_rows, carry[0])
    sel_values = jnp.where(inside[:, None, None], value_rows, carry[1])
    group = math.gcd(blocks_here, max(1, 512 // (BLK * heads_here)))
    steps_count = blocks_here // group
    span = TOPK * BLK
    position = jnp.arange(BLK, dtype=jnp.int32)
    causal = position[None, :] <= position[:, None]
    block_global = seq_here * blocks_here + jnp.arange(blocks_here, dtype=jnp.int32)
    before = my_picks < block_global[:, None]
    same = my_picks == block_global[:, None]
    allowed = my_valid[:, None, :, None] & (
        before[:, None, :, None] | same[:, None, :, None] & causal[None, :, None, :]
    )
    allowed = allowed.reshape(steps_count, group, BLK, span)
    query_steps = queries[:, 0].reshape(steps_count, group, BLK, heads_here, width)
    grad_steps = grad_out[:, 0].reshape(steps_count, group, BLK, heads_here, width)
    key_steps = sel_keys.reshape(steps_count, group, span, width)
    value_steps = sel_values.reshape(steps_count, group, span, width)
    row_steps = row_index.reshape(steps_count, group * TOPK)

    def attend(carry, inputs):
        key_acc, value_acc = carry
        q_group, do_group, k_group, v_group, mask_group, rows_group = inputs
        mask_heads = mask_group[:, None, :, :]
        scores = (
            jnp.einsum("qigw,qsw->qgis", q_group, k_group, preferred_element_type=jnp.float32)
            * scaling
        )
        highest = jnp.max(jnp.where(mask_heads, scores, -jnp.inf), axis=-1, keepdims=True)
        weights = jnp.where(mask_heads, jnp.exp(scores - highest), 0.0)
        probs = weights / jnp.sum(weights, axis=-1, keepdims=True)
        probs_b = probs.astype(jnp.bfloat16)
        dprobs = jnp.einsum("qigw,qsw->qgis", do_group, v_group, preferred_element_type=jnp.float32)
        delta = jnp.sum(probs * dprobs, axis=-1, keepdims=True)
        dscores = (probs * (dprobs - delta)).astype(jnp.bfloat16)
        query_grad = (
            jnp.einsum("qgis,qsw->qigw", dscores, k_group, preferred_element_type=jnp.float32)
            * scaling
        ).astype(jnp.bfloat16)
        key_terms = (
            jnp.einsum("qgis,qigw->qsw", dscores, q_group, preferred_element_type=jnp.float32)
            * scaling
        )
        value_terms = jnp.einsum(
            "qgis,qigw->qsw", probs_b, do_group, preferred_element_type=jnp.float32
        )
        key_acc = key_acc.at[rows_group].add(key_terms.reshape(group * TOPK, BLK * width))
        value_acc = value_acc.at[rows_group].add(value_terms.reshape(group * TOPK, BLK * width))
        return ((key_acc, value_acc), query_grad)

    zeros_dest = jnp.zeros((dest_rows, BLK * width), jnp.float32)
    (key_acc, value_acc), query_grads = lax.scan(
        attend,
        (zeros_dest, zeros_dest),
        (query_steps, grad_steps, key_steps, value_steps, allowed, row_steps),
    )
    grad_queries = query_grads.reshape(tokens, 1, heads_here, width)
    send_key_tiles = key_acc[:remote_rows].reshape(seq_count, CAP, BLK * width)
    send_value_tiles = value_acc[:remote_rows].reshape(seq_count, CAP, BLK * width)
    own_keys = key_acc[remote_rows:]
    own_values = value_acc[remote_rows:]
    choose_float = choose_out.astype(jnp.float32)
    back_keys, back_values = (
        lax.all_to_all(send_key_tiles, "seq", split_axis=0, concat_axis=0, tiled=True),
        lax.all_to_all(send_value_tiles, "seq", split_axis=0, concat_axis=0, tiled=True),
    )
    local_keys = own_keys + jnp.einsum(
        "dcb,dcx->bx", choose_float, back_keys, precision=lax.Precision.HIGHEST
    )
    local_values = own_values + jnp.einsum(
        "dcb,dcx->bx", choose_float, back_values, precision=lax.Precision.HIGHEST
    )
    total_keys, total_values = lax.psum((local_keys, local_values), "inner")
    grad_keys = total_keys.astype(jnp.bfloat16).reshape(tokens, 1, width)
    grad_values = total_values.astype(jnp.bfloat16).reshape(tokens, 1, width)
    return (grad_queries, grad_keys, grad_values)


def solution(mesh):
    return jax.shard_map(
        per_device,
        mesh=mesh,
        in_specs=(
            P(("groups", "seq"), "head", "inner", None),
            P(("groups", "seq"), "head", "inner", None),
            P(("groups", "seq"), "head", None),
            P(("groups", "seq"), "head", None),
            P("head", "groups", None),
            P("head", "groups", None),
        ),
        out_specs=(
            P(("groups", "seq"), "head", "inner", None),
            P(("groups", "seq"), "head", None),
            P(("groups", "seq"), "head", None),
        ),
        check_vma=False,
    )
```

profile of v0, /device:TPU:0, one launch (start us, length us, event | category | flops | bytes accessed | tf_op | source)
XLA Modules:
  0.0 166.9 jit_solution(11409170172867323838)
XLA Ops:
  4.3 17.6 %all_gather.6 = bf16[2048,1,128]{2,0,1:T(8,128)(2,1)S(1)} all-gather(bf16[512,1,128]{2,0,1:T(8,128)(2,1)} %param.12), channel_id=1, replica_groups=mesh['groups'=2,'seq'=4,'head'=2,'inner'=2] {'seq'}, dimensions={0}, use_global_device_ids=true | all-gather | bytes 655360 | tf_op jit(solution)/shard_map/all_gather | solution.py:52
  21.9 16.6 %all_gather.7 = bf16[2048,1,128]{2,0,1:T(8,128)(2,1)S(1)} all-gather(bf16[512,1,128]{2,0,1:T(8,128)(2,1)} %param.13), channel_id=1, replica_groups=mesh['groups'=2,'seq'=4,'head'=2,'inner'=2] {'seq'}, dimensions={0}, use_global_device_ids=true | all-gather | bytes 655360 | tf_op jit(solution)/shard_map/all_gather | solution.py:53
  39.4 2.1 %gather_fusion = bf16[128,64,128]{2,1,0:T(8,128)(2,1)} fusion(bf16[32,64,128]{2,1,0:T(8,128)(2,1)S(1)} %bitcast.131, s32[1024]{0:T(1024)S(1)} %pad_clamp_fusion), kind=kCustom, calls=%fused_computation.clone | custom fusion | bytes 4194816 | tf_op jit(solution)/shard_map/jit(_take)/gather | solution.py:58
  42.8 3.7 %select_select_fusion = (bf16[128,64,128]{2,1,0:T(8,128)(2,1)}, bf16[128,64,128]{2,1,0:T(8,128)(2,1)}) fusion(bf16[128,64,128]{2,1,0:T(8,128)(2,1)S(1)} %gather_fusion.1, pred[128]{0:T(512)(128)(4,1)S(1)} %compare_and_fusion.2, pred[128]{0:T(512)(128)(4,1)S(1)} %and.166, bf16[128,64,128]{2,1,0:T(8,128)(2,1)} %gather_fusion), kind=kLoop, calls=%fused_computation.54 | loop fusion | flops 4194304 | bytes 8388864 | tf_op jit(solution)/shard_map/jit(_where)/select_n | solution.py:61
  46.6 84.0 %while.14 = (s32[]{:T(128)}, f32[24,8192]{1,0:T(8,128)S(1)}, f32[24,8192]{1,0:T(8,128)S(1)}, bf16[4,2,64,4,128]{4,3,2,1,0:T(4,128)(2,1)}, s32[4,32]{1,0:T(4,128)...) while((s32[]{:T(128)}, f32[24,8192]{1,0:T(8,128)S(1)}, ...), condition=%wide.region_9.11_spmd, body=%wide.region_3.10_spmd.sunk | while | flops 679871104 | bytes 52703944 | solution.py:111
  52.2 1.7 %convolution_bitcast_fusion.5 = f32[2,1024,128]{2,1,0:T(8,128)} fusion(bf16[1,2,64,4,128]{4,3,2,1,0:T(4,128)(2,1)S(1)} %get-tuple-element.196, f32[2,4,64,1024]{3,2,1,0:T(8,128)S(1)} %get-tuple-element.194, f32[2,4,64]{2,1,0:T(4,128)S(1)} %get-tuple-element.195), kind=kOutput, calls=%fused_computation.16.clone.1 | convolution fusion | flops 135266304 | bytes 3278848 | tf_op jit(solution)/shard_map/while/body/eval_jaxpr/qgis,qigw->qsw/dot_general | solution.py:103
  55.3 2.1 %scatter_fusion.1 = f32[24,8192]{1,0:T(8,128)S(1)} fusion(f32[24,8192]{1,0:T(8,128)S(1)} %get-tuple-element.212, s32[32]{0:T(128)S(1)} %fusion.73, f32[32,8192]{1,0:T(8,128)S(1)} %reshape.340), kind=kCustom, calls=%fused_computation.3.clone.1 | custom fusion | flops 262144 | bytes 3145856 | tf_op jit(solution)/shard_map/while/body/eval_jaxpr/scatter-add | solution.py:107
  57.4 2.4 %fusion.76 = (f32[2,4,64]{2,1,0:T(4,128)S(1)}, f32[2,1024,64,4]{1,2,3,0:T(8,128)S(1)}) fusion(f32[2,4,64,1024]{3,2,1,0:T(8,128)} %copy-done, f32[2,4,64]{2,1,0:T(4,128)S(1)} %get-tuple-element.195, bf16[1,2,64,4,128]{4,3,2,1,0:T(4,128)(2,1)S(1)} %get-tuple-element.196, bf16[4,2,1024,128]{3,2,1,0:T(8,128)(2,1)} %get-tuple-element.229, s32[]{:T(128)S(6)} %copy.84), kind=kOutput, calls=%fused_computation.7.clone.1 | convolution fusion | flops 135790080 | bytes 4853764 | tf_op jit(solution)/shard_map/while/body/eval_jaxpr/qigw,qsw->qgis/dot_general | solution.py:92
  60.2 1.5 fusion.79
  61.7 1.5 fusion.78
  64.7 2.1 %scatter_fusion = f32[24,8192]{1,0:T(8,128)S(1)} fusion(f32[24,8192]{1,0:T(8,128)S(1)} %get-tuple-element.211, s32[32]{0:T(128)S(1)} %fusion.73, f32[32,8192]{1,0:T(8,128)S(1)} %reshape.339), kind=kCustom, calls=%fused_computation.2.clone.1 | custom fusion | flops 262144 | bytes 3145856 | tf_op jit(solution)/shard_map/while/body/eval_jaxpr/scatter-add | solution.py:106
  73.2 1.7 %convolution_bitcast_fusion.5 = f32[2,1024,128]{2,1,0:T(8,128)} fusion(bf16[1,2,64,4,128]{4,3,2,1,0:T(4,128)(2,1)S(1)} %get-tuple-element.196, f32[2,4,64,1024]{3,2,1,0:T(8,128)S(1)} %get-tuple-element.194, f32[2,4,64]{2,1,0:T(4,128)S(1)} %get-tuple-element.195), kind=kOutput, calls=%fused_computation.16.clone.1 | convolution fusion | flops 135266304 | bytes 3278848 | tf_op jit(solution)/shard_map/while/body/eval_jaxpr/qgis,qigw->qsw/dot_general | solution.py:103
  76.3 2.1 %scatter_fusion.1 = f32[24,8192]{1,0:T(8,128)S(1)} fusion(f32[24,8192]{1,0:T(8,128)S(1)} %get-tuple-element.212, s32[32]{0:T(128)S(1)} %fusion.73, f32[32,8192]{1,0:T(8,128)S(1)} %reshape.340), kind=kCustom, calls=%fused_computation.3.clone.1 | custom fusion | flops 262144 | bytes 3145856 | tf_op jit(solution)/shard_map/while/body/eval_jaxpr/scatter-add | solution.py:107
  78.4 2.4 %fusion.76 = (f32[2,4,64]{2,1,0:T(4,128)S(1)}, f32[2,1024,64,4]{1,2,3,0:T(8,128)S(1)}) fusion(f32[2,4,64,1024]{3,2,1,0:T(8,128)} %copy-done, f32[2,4,64]{2,1,0:T(4,128)S(1)} %get-tuple-element.195, bf16[1,2,64,4,128]{4,3,2,1,0:T(4,128)(2,1)S(1)} %get-tuple-element.196, bf16[4,2,1024,128]{3,2,1,0:T(8,128)(2,1)} %get-tuple-element.229, s32[]{:T(128)S(6)} %copy.84), kind=kOutput, calls=%fused_computation.7.clone.1 | convolution fusion | flops 135790080 | bytes 4853764 | tf_op jit(solution)/shard_map/while/body/eval_jaxpr/qigw,qsw->qgis/dot_general | solution.py:92
  81.2 1.5 fusion.79
  82.7 1.5 fusion.78
  85.7 2.1 %scatter_fusion = f32[24,8192]{1,0:T(8,128)S(1)} fusion(f32[24,8192]{1,0:T(8,128)S(1)} %get-tuple-element.211, s32[32]{0:T(128)S(1)} %fusion.73, f32[32,8192]{1,0:T(8,128)S(1)} %reshape.339), kind=kCustom, calls=%fused_computation.2.clone.1 | custom fusion | flops 262144 | bytes 3145856 | tf_op jit(solution)/shard_map/while/body/eval_jaxpr/scatter-add | solution.py:106
  94.2 1.7 %convolution_bitcast_fusion.5 = f32[2,1024,128]{2,1,0:T(8,128)} fusion(bf16[1,2,64,4,128]{4,3,2,1,0:T(4,128)(2,1)S(1)} %get-tuple-element.196, f32[2,4,64,1024]{3,2,1,0:T(8,128)S(1)} %get-tuple-element.194, f32[2,4,64]{2,1,0:T(4,128)S(1)} %get-tuple-element.195), kind=kOutput, calls=%fused_computation.16.clone.1 | convolution fusion | flops 135266304 | bytes 3278848 | tf_op jit(solution)/shard_map/while/body/eval_jaxpr/qgis,qigw->qsw/dot_general | solution.py:103
  97.3 2.1 %scatter_fusion.1 = f32[24,8192]{1,0:T(8,128)S(1)} fusion(f32[24,8192]{1,0:T(8,128)S(1)} %get-tuple-element.212, s32[32]{0:T(128)S(1)} %fusion.73, f32[32,8192]{1,0:T(8,128)S(1)} %reshape.340), kind=kCustom, calls=%fused_computation.3.clone.1 | custom fusion | flops 262144 | bytes 3145856 | tf_op jit(solution)/shard_map/while/body/eval_jaxpr/scatter-add | solution.py:107
  99.4 2.4 %fusion.76 = (f32[2,4,64]{2,1,0:T(4,128)S(1)}, f32[2,1024,64,4]{1,2,3,0:T(8,128)S(1)}) fusion(f32[2,4,64,1024]{3,2,1,0:T(8,128)} %copy-done, f32[2,4,64]{2,1,0:T(4,128)S(1)} %get-tuple-element.195, bf16[1,2,64,4,128]{4,3,2,1,0:T(4,128)(2,1)S(1)} %get-tuple-element.196, bf16[4,2,1024,128]{3,2,1,0:T(8,128)(2,1)} %get-tuple-element.229, s32[]{:T(128)S(6)} %copy.84), kind=kOutput, calls=%fused_computation.7.clone.1 | convolution fusion | flops 135790080 | bytes 4853764 | tf_op jit(solution)/shard_map/while/body/eval_jaxpr/qigw,qsw->qgis/dot_general | solution.py:92
  103.7 1.5 fusion.78
  106.7 2.1 %scatter_fusion = f32[24,8192]{1,0:T(8,128)S(1)} fusion(f32[24,8192]{1,0:T(8,128)S(1)} %get-tuple-element.211, s32[32]{0:T(128)S(1)} %fusion.73, f32[32,8192]{1,0:T(8,128)S(1)} %reshape.339), kind=kCustom, calls=%fused_computation.2.clone.1 | custom fusion | flops 262144 | bytes 3145856 | tf_op jit(solution)/shard_map/while/body/eval_jaxpr/scatter-add | solution.py:106
  115.2 1.7 %convolution_bitcast_fusion.5 = f32[2,1024,128]{2,1,0:T(8,128)} fusion(bf16[1,2,64,4,128]{4,3,2,1,0:T(4,128)(2,1)S(1)} %get-tuple-element.196, f32[2,4,64,1024]{3,2,1,0:T(8,128)S(1)} %get-tuple-element.194, f32[2,4,64]{2,1,0:T(4,128)S(1)} %get-tuple-element.195), kind=kOutput, calls=%fused_computation.16.clone.1 | convolution fusion | flops 135266304 | bytes 3278848 | tf_op jit(solution)/shard_map/while/body/eval_jaxpr/qgis,qigw->qsw/dot_general | solution.py:103
  118.3 2.1 %scatter_fusion.1 = f32[24,8192]{1,0:T(8,128)S(1)} fusion(f32[24,8192]{1,0:T(8,128)S(1)} %get-tuple-element.212, s32[32]{0:T(128)S(1)} %fusion.73, f32[32,8192]{1,0:T(8,128)S(1)} %reshape.340), kind=kCustom, calls=%fused_computation.3.clone.1 | custom fusion | flops 262144 | bytes 3145856 | tf_op jit(solution)/shard_map/while/body/eval_jaxpr/scatter-add | solution.py:107
  120.4 2.4 %fusion.76 = (f32[2,4,64]{2,1,0:T(4,128)S(1)}, f32[2,1024,64,4]{1,2,3,0:T(8,128)S(1)}) fusion(f32[2,4,64,1024]{3,2,1,0:T(8,128)} %copy-done, f32[2,4,64]{2,1,0:T(4,128)S(1)} %get-tuple-element.195, bf16[1,2,64,4,128]{4,3,2,1,0:T(4,128)(2,1)S(1)} %get-tuple-element.196, bf16[4,2,1024,128]{3,2,1,0:T(8,128)(2,1)} %get-tuple-element.229, s32[]{:T(128)S(6)} %copy.84), kind=kOutput, calls=%fused_computation.7.clone.1 | convolution fusion | flops 135790080 | bytes 4853764 | tf_op jit(solution)/shard_map/while/body/eval_jaxpr/qigw,qsw->qgis/dot_general | solution.py:92
  124.7 1.5 fusion.78
  127.7 2.1 %scatter_fusion = f32[24,8192]{1,0:T(8,128)S(1)} fusion(f32[24,8192]{1,0:T(8,128)S(1)} %get-tuple-element.211, s32[32]{0:T(128)S(1)} %fusion.73, f32[32,8192]{1,0:T(8,128)S(1)} %reshape.339), kind=kCustom, calls=%fused_computation.2.clone.1 | custom fusion | flops 262144 | bytes 3145856 | tf_op jit(solution)/shard_map/while/body/eval_jaxpr/scatter-add | solution.py:106
  131.5 4.1 %all-to-all-start = ((f32[4,4,8192]{2,1,0:T(4,128)}), f32[4,4,8192]{2,1,0:T(4,128)S(1)}, u32[]{:S(2)}, u32[]{:S(2)}) async-start(f32[4,4,8192]{2,1,0:T(4,128)} %reshape.280), calls=%async_computation | async-start | bytes 1048576 | tf_op jit(solution)/shard_map/all_to_all | solution.py:123
  137.0 8.9 %all-to-all-done = f32[4,4,8192]{2,1,0:T(4,128)S(1)} async-done(((f32[4,4,8192]{2,1,0:T(4,128)}), f32[4,4,8192]{2,1,0:T(4,128)S(1)}, u32[]{:S(2)}, u32[]{:S(2)}) %all-to-all-start) | async-done | bytes 524320 | tf_op jit(solution)/shard_map/all_to_all | solution.py:123
  146.0 3.5 %all-to-all-start.1 = ((f32[4,4,8192]{2,1,0:T(4,128)}), f32[4,4,8192]{2,1,0:T(4,128)S(1)}, u32[]{:S(2)}, u32[]{:S(2)}) async-start(f32[4,4,8192]{2,1,0:T(4,128)} %reshape.282), calls=%async_computation.1 | async-start | bytes 1048576 | tf_op jit(solution)/shard_map/all_to_all | solution.py:124
  150.7 9.0 %all-to-all-done.1 = f32[4,4,8192]{2,1,0:T(4,128)S(1)} async-done(((f32[4,4,8192]{2,1,0:T(4,128)}), f32[4,4,8192]{2,1,0:T(4,128)S(1)}, u32[]{:S(2)}, u32[]{:S(2)}) %all-to-all-start.1) | async-done | bytes 524320 | tf_op jit(solution)/shard_map/all_to_all | solution.py:124
  160.6 4.8 %all-reduce.2 = (bf16[8,8192]{1,0:T(8,128)(2,1)S(1)}, bf16[8,8192]{1,0:T(8,128)(2,1)S(1)}) all-reduce(f32[8,8192]{1,0:T(8,128)S(1)} %fusion.30, f32[8,8192]{1,0:T(8,128)S(1)} %fusion.31), channel_id=1, replica_groups=mesh['groups'=2,'seq'=4,'head'=2,'inner'=2] {'inner'}, use_global_device_ids=true, to_apply=%region_12.14 | all-reduce | flops 131072 | bytes 786432 | tf_op jit(solution)/shard_map/psum | solution.py:132
  (109 shorter events, 53.0 us)
Async XLA Ops:
  50.9 1.3 copy-start
  57.4 2.4 %copy-start.1 = (f32[2,4,64,1024]{3,2,1,0:T(8,128)S(1)}, f32[2,4,64,1024]{3,2,1,0:T(8,128)}, u32[]{:S(2)}) copy-start(f32[2,4,64,1024]{3,2,1,0:T(8,128)} %copy-done) | copy-start | bytes 6291460 | tf_op jit(solution)/shard_map/while
  71.9 1.3 copy-start
  78.4 2.4 %copy-start.1 = (f32[2,4,64,1024]{3,2,1,0:T(8,128)S(1)}, f32[2,4,64,1024]{3,2,1,0:T(8,128)}, u32[]{:S(2)}) copy-start(f32[2,4,64,1024]{3,2,1,0:T(8,128)} %copy-done) | copy-start | bytes 6291460 | tf_op jit(solution)/shard_map/while
  92.9 1.3 copy-start
  99.4 2.4 %copy-start.1 = (f32[2,4,64,1024]{3,2,1,0:T(8,128)S(1)}, f32[2,4,64,1024]{3,2,1,0:T(8,128)}, u32[]{:S(2)}) copy-start(f32[2,4,64,1024]{3,2,1,0:T(8,128)} %copy-done) | copy-start | bytes 6291460 | tf_op jit(solution)/shard_map/while
  113.9 1.3 copy-start
  120.4 2.4 %copy-start.1 = (f32[2,4,64,1024]{3,2,1,0:T(8,128)S(1)}, f32[2,4,64,1024]{3,2,1,0:T(8,128)}, u32[]{:S(2)}) copy-start(f32[2,4,64,1024]{3,2,1,0:T(8,128)} %copy-done) | copy-start | bytes 6291460 | tf_op jit(solution)/shard_map/while
  131.5 14.4 %all-to-all-start = ((f32[4,4,8192]{2,1,0:T(4,128)}), f32[4,4,8192]{2,1,0:T(4,128)S(1)}, u32[]{:S(2)}, u32[]{:S(2)}) async-start(f32[4,4,8192]{2,1,0:T(4,128)} %reshape.280), calls=%async_computation | async-start | bytes 1048576 | tf_op jit(solution)/shard_map/all_to_all | solution.py:123
  146.0 13.7 %all-to-all-start.1 = ((f32[4,4,8192]{2,1,0:T(4,128)}), f32[4,4,8192]{2,1,0:T(4,128)S(1)}, u32[]{:S(2)}, u32[]{:S(2)}) async-start(f32[4,4,8192]{2,1,0:T(4,128)} %reshape.282), calls=%async_computation.1 | async-start | bytes 1048576 | tf_op jit(solution)/shard_map/all_to_all | solution.py:124
where the time goes:
time: 168 us; the launch traced here: 167 us
  blocking collectives  39 us (23%)
  local copies, waits for them, and re-layouts  37.2 us (22%)
  matrix products  36.2 us (22%)
  other arithmetic  27.9 us (17%)
  waiting for transfers between devices  17.9 us (11%)
  starting transfers between devices  7.61 us (5%)
    all_gather x1, blocking collectives, per_device(): key_piece = lax.all_gather(keys, 'seq', axis=0, tiled=True)  17.6 us
    all_gather x1, blocking collectives, per_device(): value_piece = lax.all_gather(values, 'seq', axis=0, tiled=True)  16.6 us
    dot_general x4, matrix products, attend(): jnp.einsum('qigw,qsw->qgis', do_group, v_group, preferred_element_type=jn...  9.67 us
    all_to_all x1, waiting for transfers between devices, per_device(): lax.all_to_all(send_value_tiles, 'seq', split_axis=0, concat_axis=0, tile...  9 us
    all_to_all x1, waiting for transfers between devices, per_device(): lax.all_to_all(send_key_tiles, 'seq', split_axis=0, concat_axis=0, tiled=...  8.93 us
    scatter-add x4, other arithmetic, attend(): value_acc.at[rows_group].add(value_terms.reshape(group * TOPK, BLK * width))  8.42 us
    scatter-add x4, other arithmetic, attend(): key_acc.at[rows_group].add(key_terms.reshape(group * TOPK, BLK * width))  8.42 us
    dot_general x4, matrix products, attend(): jnp.einsum('qgis,qigw->qsw', probs_b, do_group, preferred_element_type=jn...  6.69 us
  transfers between devices with their start and end apart: 2, of which 2 were waited for; matrix products, arithmetic and copies ran while one was open for 2% of the time, Pallas kernels for 0%

commit v1 on v0

v1 whole, which is shorter than its diff:
```python
import functools
import math

import jax
import jax.numpy as jnp
from jax import lax
from jax.experimental import pallas as pl
from jax.experimental.pallas import tpu as pltpu
from jax.sharding import PartitionSpec as P

BLK = 64
CAP = 4
NEG = -1e30
F32 = jnp.float32
BF16 = jnp.bfloat16
NT = (((1,), (1,)), ((), ()))
TN = (((0,), (0,)), ((), ()))


def dot(a, b, dims=(((1,), (0,)), ((), ()))):
    return lax.dot_general(a, b, dims, preferred_element_type=F32)


def vmem():
    return pl.BlockSpec(memory_space=pltpu.VMEM)


def smem():
    return pl.BlockSpec(memory_space=pltpu.SMEM)


def whole(shape):
    return pl.BlockSpec(shape, lambda b: (0,) * len(shape))


def prep_kernel(idx_ref, valid_ref, k_ref, v_ref, lim_ref, send_ref, *rest, runs, here):
    packs, hit_ref = rest[:-1], rest[-1]
    seq = lax.axis_index("seq")
    inner = lax.axis_index("inner")
    slots, total = idx_ref.shape
    named = jnp.where(valid_ref[...] > 0, idx_ref[...], -1)
    block = lax.broadcasted_iota(jnp.int32, (total, total), 0)
    hit = jnp.zeros((total, total), jnp.int32)
    for t in range(slots):
        hit = jnp.where(named[t : t + 1, :] == block, 1, hit)
    hit_ref[...] = hit
    lane = lax.broadcasted_iota(jnp.int32, (here, total), 1)
    row = lax.broadcasted_iota(jnp.int32, (here, total), 0)
    lane_run = lane // here
    wide = lax.broadcasted_iota(jnp.int32, (here, 128), 1)
    tall = lax.broadcasted_iota(jnp.int32, (here, 128), 0)

    def ranks(hits, run):
        present = jnp.max(jnp.where(lane_run == run, hits, 0), axis=1, keepdims=True)
        present = jnp.broadcast_to(present, (here, 128))
        count = present
        step = 1
        while step < here:
            count = count + jnp.where(tall >= step, pltpu.roll(count, step, 0), 0)
            step *= 2
        return present, count - present

    own = hit_ref[pl.ds(pl.multiple_of(seq * here, here), here), :]
    lim_ref[0:here, 0:total] = jnp.where(own > 0, jnp.where(lane == row + seq * here, 0, BLK), -2 * BLK)
    for d in range(1, runs):
        source = jnp.maximum(seq - d, 0)
        hits = hit_ref[pl.ds(pl.multiple_of(source * here, here), here), :]
        present, rank = ranks(hits, seq)
        rank = jnp.where((present > 0) & (seq >= d), rank, -1)[:, 0:1]
        for c in range(CAP):
            picked = jnp.max(jnp.where(rank == c, hits, 0), axis=0, keepdims=True)
            at = here + (d - 1) * CAP + c
            lim_ref[at : at + 1, 0:total] = jnp.where(picked > 0, BLK, -2 * BLK)
    rows = jnp.where(inner == 0, k_ref[...].astype(F32), v_ref[...].astype(F32))
    for d in range(1, runs):
        present, rank = ranks(own, seq + d)
        place = jnp.where((present > 0) & (rank == wide), tall, 0)
        place = jnp.sum(place, axis=0, keepdims=True)
        send_ref[d - 1 : d, :] = place
        for c in range(CAP):
            which = jnp.broadcast_to(place[:, c : c + 1], (BLK, 128))
            tile = rows[0:BLK]
            for n in range(1, here):
                tile = jnp.where(which == n, rows[n * BLK : (n + 1) * BLK], tile)
            packs[d - 1][c * BLK : (c + 1) * BLK, :] = tile.astype(BF16)


def masked(s, lim_ref, first, query, diff):
    tiles = []
    for j in range(s.shape[0] // BLK):
        limit = lim_ref[first + j, query]
        tile = s[j * BLK : (j + 1) * BLK]
        keep = diff <= limit
        tiles.append(jnp.where(keep, tile, NEG))
    return jnp.concatenate(tiles, axis=0)


def key_minus_token(heads):
    shape = (BLK, BLK * heads)
    return lax.broadcasted_iota(jnp.int32, shape, 0) - lax.broadcasted_iota(jnp.int32, shape, 1) // heads


def own_stats_kernel(lim_ref, q_ref, do_ref, k_ref, v_ref, stat_ref, *, heads, here, factor):
    query = lax.axis_index("seq") * here + pl.program_id(0)
    s = dot(k_ref[...], q_ref[...], NT)
    s = masked(s, lim_ref, 0, query, key_minus_token(heads))
    top = jnp.max(s, axis=0, keepdims=True)
    w = jnp.exp2((s - top) * factor)
    dp = dot(v_ref[...], do_ref[...], NT)
    stat_ref[0, 0:1, :] = top
    stat_ref[0, 1:2, :] = jnp.sum(w, axis=0, keepdims=True)
    stat_ref[0, 2:3, :] = jnp.sum(w * dp, axis=0, keepdims=True)


def remote_kernel(lim_ref, q_ref, do_ref, stat_ref, *refs, heads, here, away, factor, scaling):
    direct, swapped = refs[:away], refs[away : 2 * away]
    ds_ref, keep_ref, send_ref, kr_ref, out_stat_ref, vr_ref, dk_ref, dv_ref = refs[2 * away :]
    step = pl.program_id(0)
    inner = lax.axis_index("inner")
    query = lax.axis_index("seq") * here + step
    span = CAP * BLK

    @pl.when(step == 0)
    def _():
        for d in range(away):
            first = jnp.where(inner == 0, direct[d][...].astype(F32), swapped[d][...].astype(F32))
            second = jnp.where(inner == 0, swapped[d][...].astype(F32), direct[d][...].astype(F32))
            kr_ref[d * span : (d + 1) * span, :] = first.astype(BF16)
            vr_ref[d * span : (d + 1) * span, :] = second.astype(BF16)
        dk_ref[...] = jnp.zeros_like(dk_ref)
        dv_ref[...] = jnp.zeros_like(dv_ref)

    q = q_ref[...]
    do = do_ref[...]
    s = dot(kr_ref[...], q, NT)
    tiles = []
    for j in range(away * CAP):
        tile = s[j * BLK : (j + 1) * BLK]
        tiles.append(jnp.where(lim_ref[here + j, query] > 0, tile, NEG))
    s = jnp.concatenate(tiles, axis=0)
    own_top = stat_ref[0, 0:1, :]
    top = jnp.maximum(own_top, jnp.max(s, axis=0, keepdims=True))
    shrink = jnp.exp2((own_top - top) * factor)
    w = jnp.exp2((s - top) * factor)
    dp = dot(vr_ref[...], do, NT)
    total = stat_ref[0, 1:2, :] * shrink + jnp.sum(w, axis=0, keepdims=True)
    delta = stat_ref[0, 2:3, :] * shrink + jnp.sum(w * dp, axis=0, keepdims=True)
    inverse = 1.0 / total
    delta = delta * inverse
    p = w * inverse
    ds = (p * (dp - delta)).astype(BF16)
    ds_ref[...] = ds
    dk_ref[...] += dot(ds, q)
    dv_ref[...] += dot(p.astype(BF16), do)
    out_stat_ref[0, 0:1, :] = top
    out_stat_ref[0, 1:2, :] = inverse
    out_stat_ref[0, 2:3, :] = delta

    @pl.when(step == pl.num_programs(0) - 1)
    def _():
        store_split(inner, dk_ref, dv_ref, keep_ref, send_ref, scaling)


def store_split(inner, dk_ref, dv_ref, keep_ref, send_ref, scaling):
    @pl.when(inner == 0)
    def _():
        keep_ref[...] = dk_ref[...] * scaling
        send_ref[...] = dv_ref[...]

    @pl.when(inner != 0)
    def _():
        keep_ref[...] = dv_ref[...]
        send_ref[...] = dk_ref[...] * scaling


def own_grads_kernel(
    lim_ref, q_ref, do_ref, k_ref, v_ref, kr_ref, ds_ref, stat_ref,
    dq_ref, keep_ref, send_ref, dk_ref, dv_ref, *, heads, here, factor, scaling,
):
    step = pl.program_id(0)
    inner = lax.axis_index("inner")
    query = lax.axis_index("seq") * here + step

    @pl.when(step == 0)
    def _():
        dk_ref[...] = jnp.zeros_like(dk_ref)
        dv_ref[...] = jnp.zeros_like(dv_ref)

    q = q_ref[...]
    do = do_ref[...]
    k = k_ref[...]
    s = dot(k, q, NT)
    s = masked(s, lim_ref, 0, query, key_minus_token(heads))
    p = jnp.exp2((s - stat_ref[0, 0:1, :]) * factor) * stat_ref[0, 1:2, :]
    dp = dot(v_ref[...], do, NT)
    ds = (p * (dp - stat_ref[0, 2:3, :])).astype(BF16)
    dk_ref[...] += dot(ds, q)
    dv_ref[...] += dot(p.astype(BF16), do)
    dq = dot(k, ds, TN) + dot(kr_ref[...], ds_ref[...], TN)
    dq_ref[...] = (dq * scaling).T.astype(BF16)

    @pl.when(step == pl.num_programs(0) - 1)
    def _():
        store_split(inner, dk_ref, dv_ref, keep_ref, send_ref, scaling)


def combine_kernel(send_ref, keep_ref, recv_ref, *refs, away):
    arrived, out_ref, acc_ref = refs[:away], refs[away], refs[away + 1]
    seq = lax.axis_index("seq")
    acc_ref[...] = keep_ref[...] + recv_ref[...]
    for d in range(1, away + 1):

        @pl.when(seq + d <= away)
        def _():
            for c in range(CAP):
                at = pl.ds(pl.multiple_of(send_ref[d - 1, c] * BLK, BLK), BLK)
                acc_ref[at, :] += arrived[d - 1][c * BLK : (c + 1) * BLK, :].astype(F32)

    out_ref[...] = acc_ref[...].astype(BF16)


def per_device(queries, grad_out, keys, values, indices, valid):
    tokens, _, heads, width = queries.shape
    runs = lax.axis_size("seq")
    away = runs - 1
    inner = lax.axis_index("inner")
    here = tokens // BLK
    total = indices.shape[1]
    scaling = 1.0 / math.sqrt(width)
    factor = scaling * math.log2(math.e)
    rows = BLK * heads
    span = CAP * BLK
    far = away * span
    lanes = -(-total // 128) * 128
    swap = [(0, 1), (1, 0)]
    q = queries.reshape(tokens * heads, width)
    do = grad_out.reshape(tokens * heads, width)
    k = keys.reshape(tokens, width)
    v = values.reshape(tokens, width)
    lim, send, *packs = pl.pallas_call(
        functools.partial(prep_kernel, runs=runs, here=here),
        in_specs=[vmem()] * 4,
        out_specs=[vmem()] * (2 + away),
        out_shape=[
            jax.ShapeDtypeStruct((here + away * CAP, lanes), jnp.int32),
            jax.ShapeDtypeStruct((away, 128), jnp.int32),
        ]
        + [jax.ShapeDtypeStruct((span, width), BF16)] * away,
        scratch_shapes=[pltpu.VMEM((total, total), jnp.int32)],
        name="prep",
    )(indices[0].T, valid[0].T, k, v)
    direct = [
        lax.ppermute(packs[d - 1], "seq", [(s, (s + d) % runs) for s in range(runs)])
        for d in range(1, runs)
    ]
    row_block = pl.BlockSpec((rows, width), lambda b: (b, 0))
    stat_block = pl.BlockSpec((1, 8, rows), lambda b: (b, 0, 0))
    stat_shape = jax.ShapeDtypeStruct((here, 8, rows), F32)
    own_stats = pl.pallas_call(
        functools.partial(own_stats_kernel, heads=heads, here=here, factor=factor),
        grid=(here,),
        in_specs=[smem(), row_block, row_block, whole((tokens, width)), whole((tokens, width))],
        out_specs=stat_block,
        out_shape=stat_shape,
        name="own_stats",
        cost_estimate=pl.CostEstimate(flops=10**9, transcendentals=10**6, bytes_accessed=10**6),
    )(lim, q, do, k, v)
    swapped = [lax.ppermute(x, "inner", swap) for x in direct]
    ds_far, keep_far, send_far, k_far, stats = pl.pallas_call(
        functools.partial(
            remote_kernel, heads=heads, here=here, away=away, factor=factor, scaling=scaling
        ),
        grid=(here,),
        in_specs=[smem(), row_block, row_block, stat_block] + [whole((span, width))] * (2 * away),
        out_specs=[
            pl.BlockSpec((far, rows), lambda b: (0, b)),
            whole((far, width)),
            whole((far, width)),
            whole((far, width)),
            stat_block,
        ],
        out_shape=[
            jax.ShapeDtypeStruct((far, tokens * heads), BF16),
            jax.ShapeDtypeStruct((far, width), F32),
            jax.ShapeDtypeStruct((far, width), F32),
            jax.ShapeDtypeStruct((far, width), BF16),
            stat_shape,
        ],
        scratch_shapes=[
            pltpu.VMEM((far, width), BF16),
            pltpu.VMEM((far, width), F32),
            pltpu.VMEM((far, width), F32),
        ],
        name="far_grads",
        cost_estimate=pl.CostEstimate(flops=2 * 10**9, transcendentals=10**6, bytes_accessed=10**6),
    )(lim, q, do, own_stats, *direct, *swapped)
    from_peer = lax.ppermute(send_far, "inner", swap)
    summed = (keep_far + from_peer).astype(BF16)
    arrived = [
        lax.ppermute(
            summed[(d - 1) * span : d * span], "seq", [(r, (r - d) % runs) for r in range(runs)]
        )
        for d in range(1, runs)
    ]
    grad_queries, keep_own, send_own = pl.pallas_call(
        functools.partial(
            own_grads_kernel, heads=heads, here=here, factor=factor, scaling=scaling
        ),
        grid=(here,),
        in_specs=[
            smem(),
            row_block,
            row_block,
            whole((tokens, width)),
            whole((tokens, width)),
            whole((far, width)),
            pl.BlockSpec((far, rows), lambda b: (0, b)),
            stat_block,
        ],
        out_specs=[row_block, whole((tokens, width)), whole((tokens, width))],
        out_shape=[
            jax.ShapeDtypeStruct((tokens * heads, width), BF16),
            jax.ShapeDtypeStruct((tokens, width), F32),
            jax.ShapeDtypeStruct((tokens, width), F32),
        ],
        scratch_shapes=[pltpu.VMEM((tokens, width), F32), pltpu.VMEM((tokens, width), F32)],
        name="own_grads",
        cost_estimate=pl.CostEstimate(flops=2 * 10**9, transcendentals=10**6, bytes_accessed=10**6),
    )(lim, q, do, k, v, k_far, ds_far, stats)
    own_peer = lax.ppermute(send_own, "inner", swap)
    mine = pl.pallas_call(
        functools.partial(combine_kernel, away=away),
        in_specs=[smem(), vmem(), vmem()] + [vmem()] * away,
        out_specs=vmem(),
        out_shape=jax.ShapeDtypeStruct((tokens, width), BF16),
        scratch_shapes=[pltpu.VMEM((tokens, width), F32)],
        name="combine",
    )(send, keep_own, own_peer, *arrived)
    other = lax.ppermute(mine, "inner", swap)
    grad_keys = jnp.where(inner == 0, mine, other).reshape(tokens, 1, width)
    grad_values = jnp.where(inner == 0, other, mine).reshape(tokens, 1, width)
    return (grad_queries.reshape(tokens, 1, heads, width), grad_keys, grad_values)


def solution(mesh):
    return jax.shard_map(
        per_device,
        mesh=mesh,
        in_specs=(
            P(("groups", "seq"), "head", "inner", None),
            P(("groups", "seq"), "head", "inner", None),
            P(("groups", "seq"), "head", None),
            P(("groups", "seq"), "head", None),
            P("head", "groups", None),
            P("head", "groups", None),
        ),
        out_specs=(
            P(("groups", "seq"), "head", "inner", None),
            P(("groups", "seq"), "head", None),
            P(("groups", "seq"), "head", None),
        ),
        check_vma=False,
    )
```

time: 168 us -> 59.6 us (0.35)
  blocking collectives: 39 us -> 0 us
  matrix products: 36.2 us -> 0 us
  local copies, waits for them, and re-layouts: 37.2 us -> 1.85 us
  Pallas kernels: 0 us -> 31.5 us
  other arithmetic: 27.9 us -> 1.67 us
  waiting for transfers between devices: 17.9 us -> 11.3 us
  starting transfers between devices: 7.61 us -> 11.8 us
    dot_general x22 -> x0, matrix products: 36.2 us -> none  [the longest x4 9.67 us: attend(): jnp.einsum('qigw,qsw->qgis', do_group, v_group, preferred_element_type=jn...]
    all_gather x2 -> x0, blocking collectives: 34.1 us -> none  [the longest x1 17.6 us: per_device(): key_piece = lax.all_gather(keys, 'seq', axis=0, tiled=True)]
    pallas_call x0 -> x5, Pallas kernels: none -> 31.5 us  [the longest x1 11.5 us: per_device(): pl.pallas_call(functools.partial(remote_kernel, heads=heads, here=here, a...]
    all_to_all x2 -> x0, waiting for transfers between devices: 17.9 us -> none  [the longest x1 9 us: per_device(): lax.all_to_all(send_value_tiles, 'seq', split_axis=0, concat_axis=0, tile...]
    scatter-add x8 -> x0, other arithmetic: 16.8 us -> none  [the longest x4 8.42 us: attend(): value_acc.at[rows_group].add(value_terms.reshape(group * TOPK, BLK * width))]
    reshape x13 -> x0, local copies, waits for them, and re-layouts: 14.7 us -> none  [the longest x4 5.66 us: attend(): value_terms.reshape(group * TOPK, BLK * width)]
    ppermute x0 -> x12, starting transfers between devices: none -> 11.8 us  [the longest x3 6.99 us: per_device(): lax.ppermute(packs[d - 1], 'seq', [(s, (s + d) % runs) for s in range(run...]
    ppermute x0 -> x12, waiting for transfers between devices: none -> 11.3 us  [the longest x3 6.18 us: per_device(): lax.ppermute(summed[(d - 1) * span:d * span], 'seq', [(r, (r - d) % runs)...]
  transfers between devices with their start and end apart: 2 -> 12, of which waited for: 2 -> 7; matrix products, arithmetic and copies ran while one was open for 2% -> 0% of each run, Pallas kernels for 0% -> 27%
where the time goes in v1:
time: 59.6 us; the launch traced here: 58.9 us
  Pallas kernels  31.5 us (53%)
  starting transfers between devices  11.8 us (20%)
  waiting for transfers between devices  11.3 us (19%)
  local copies, waits for them, and re-layouts  1.85 us (3%)
  other arithmetic  1.67 us (3%)
  between operations  0.73 us (1%)
    pallas_call x1, Pallas kernels, per_device(): pl.pallas_call(functools.partial(remote_kernel, heads=heads, here=here, a...  11.5 us
    pallas_call x1, Pallas kernels, per_device(): pl.pallas_call(functools.partial(own_grads_kernel, heads=heads, here=here...  9.46 us
    ppermute x3, starting transfers between devices, per_device(): lax.ppermute(packs[d - 1], 'seq', [(s, (s + d) % runs) for s in range(run...  6.99 us
    pallas_call x1, Pallas kernels, per_device(): pl.pallas_call(functools.partial(own_stats_kernel, heads=heads, here=here...  6.74 us
    ppermute x3, waiting for transfers between devices, per_device(): lax.ppermute(summed[(d - 1) * span:d * span], 'seq', [(r, (r - d) % runs)...  6.18 us
    ppermute x3, starting transfers between devices, per_device(): lax.ppermute(summed[(d - 1) * span:d * span], 'seq', [(r, (r - d) % runs)...  3.88 us
    ppermute x3, waiting for transfers between devices, per_device(): lax.ppermute(packs[d - 1], 'seq', [(s, (s + d) % runs) for s in range(run...  3.57 us
    pallas_call x1, Pallas kernels, per_device(): pl.pallas_call(functools.partial(prep_kernel, runs=runs, here=here), in_s...  2.04 us
  transfers between devices with their start and end apart: 12, of which 7 were waited for; matrix products, arithmetic and copies ran while one was open for 0% of the time, Pallas kernels for 27%

profile of v1, /device:TPU:0, one launch (start us, length us, event | category | flops | bytes accessed | tf_op | source)
XLA Modules:
  0.0 58.9 jit_solution(16043908103773436663)
XLA Ops:
  0.6 2.0 %prep.1 = (s32[20,128]{1,0:T(8,128)}, s32[3,128]{1,0:T(4,128)}, bf16[256,128]{1,0:T(8,128)(2,1)}, bf16[256,128]{1,0:T(8,128)(2,1)}, bf16[256,128]{1,0:T(8,128)(2,1)}) custom-call(s32[16,32]{1,0:T(8,128)} %bitcast.23, s32[16,32]{1,0:T(8,128)} %bitcast.24, bf16[512,128]{1,0:T(8,128)(2,1)} %bitcast.17, bf16[512,128]{1,0:T(8,128)(2,1)} %bitcast.20), custom_call_target="tpu_custom_call" | custom-call | tf_op jit(solution)/shard_map/prep/pallas_call | solution.py:240
  2.7 3.1 %collective-permute-start = (bf16[256,128]{1,0:T(8,128)(2,1)}, bf16[256,128]{1,0:T(8,128)(2,1)S(1)}, u32[]{:S(2)}, u32[]{:S(2)}) collective-permute-start(bf16[256,128]{1,0:T(8,128)(2,1)} %get-tuple-element.17), channel_id=1, source_target_pairs={{0,4},{4,8},{8,12},{12,0},{1,5},{5,9},{9,13},{13,1},{2,6},{6,10},{... | collective-permute-start | bytes 196616 | tf_op jit(solution)/shard_map/ppermute | solution.py:253
  5.7 2.6 %collective-permute-start.1 = (bf16[256,128]{1,0:T(8,128)(2,1)}, bf16[256,128]{1,0:T(8,128)(2,1)S(1)}, u32[]{:S(2)}, u32[]{:S(2)}) collective-permute-start(bf16[256,128]{1,0:T(8,128)(2,1)} %get-tuple-element.18), channel_id=1, source_target_pairs={{0,8},{4,12},{8,0},{12,4},{1,9},{5,13},{9,1},{13,5},{2,10},{6,14},... | collective-permute-start | bytes 196616 | tf_op jit(solution)/shard_map/ppermute | solution.py:253
  8.3 1.3 %collective-permute-start.2 = (bf16[256,128]{1,0:T(8,128)(2,1)}, bf16[256,128]{1,0:T(8,128)(2,1)S(1)}, u32[]{:S(2)}, u32[]{:S(2)}) collective-permute-start(bf16[256,128]{1,0:T(8,128)(2,1)} %get-tuple-element.19), channel_id=1, source_target_pairs={{0,12},{4,0},{8,4},{12,8},{1,13},{5,1},{9,5},{13,9},{2,14},{6,2},{... | collective-permute-start | bytes 196616 | tf_op jit(solution)/shard_map/ppermute | solution.py:253
  9.7 0.8 %collective-permute-done.refs_0_ = bf16[256,128]{1,0:T(8,128)(2,1)S(1)} collective-permute-done((bf16[256,128]{1,0:T(8,128)(2,1)}, bf16[256,128]{1,0:T(8,128)(2,1)S(1)}, u32[]{:S(2)}, u32[]{:S(2)}) %collective-permute-start) | collective-permute-done | bytes 65568 | tf_op jit(solution)/shard_map/ppermute | solution.py:253
  10.4 0.0 collective-permute-start.3
  10.4 2.6 %collective-permute-done.1.refs_1_ = bf16[256,128]{1,0:T(8,128)(2,1)S(1)} collective-permute-done((bf16[256,128]{1,0:T(8,128)(2,1)}, bf16[256,128]{1,0:T(8,128)(2,1)S(1)}, u32[]{:S(2)}, u32[]{:S(2)}) %collective-permute-start.1) | collective-permute-done | bytes 65568 | tf_op jit(solution)/shard_map/ppermute | solution.py:253
  13.0 0.0 collective-permute-start.4
  13.0 0.2 collective-permute-done.2.refs_2_
  13.2 0.3 collective-permute-start.5
  13.5 6.7 %own_stats.1.stat_ref = f32[8,8,256]{2,1,0:T(8,128)} custom-call(s32[20,128]{1,0:T(8,128)} %get-tuple-element.16.lim_ref, bf16[2048,128]{1,0:T(8,128)(2,1)} %bitcast.25, bf16[2048,128]{1,0:T(8,128)(2,1)} %bitcast.28, bf16[512,128]{1,0:T(8,128)(2,1)} %bitcast.18, bf16[512,128]{1,0:T(8,128)(2,1)} %bitcast.21), custom_call_target="tpu_custom_call" | custom-call | flops 1000000000 | bytes 1000000 | tf_op jit(solution)/shard_map/own_stats/pallas_call | solution.py:259
  20.3 0.0 collective-permute-done.3.refs_3_
  20.3 0.0 collective-permute-done.4.refs_4_
  20.3 0.0 collective-permute-done.5.refs_5_
  20.3 0.5 copy-done.8
  20.9 0.0 copy-done.9
  20.9 0.6 %copy-done.10 = bf16[256,128]{1,0:T(8,128)(2,1)} copy-done((bf16[256,128]{1,0:T(8,128)(2,1)}, bf16[256,128]{1,0:T(8,128)(2,1)S(1)}, u32[]{:S(2)}) %copy-start.10) | copy-done | bytes 65560
  21.5 11.5 %far_grads.1 = (bf16[768,2048]{1,0:T(8,128)(2,1)}, f32[768,128]{1,0:T(8,128)}, f32[768,128]{1,0:T(8,128)}, bf16[768,128]{1,0:T(8,128)(2,1)}, f32[8,8,256]{2,1,0:T(8,128)}) custom-call(s32[20,128]{1,0:T(8,128)} %get-tuple-element.16.lim_ref, bf16[2048,128]{1,0:T(8,128)(2,1)} %bitcast.26, bf16[2048,128]{1,0:T(8,128)(2,1)} %bitcast.29, ...), custom_call_target="tpu_custom_call" | custom-call | flops 2000000000 | bytes 1000000 | tf_op jit(solution)/shard_map/far_grads/pallas_call | solution.py:269
  33.0 0.3 collective-permute-start.7
  33.3 9.5 %own_grads.1 = (bf16[2048,128]{1,0:T(8,128)(2,1)}, f32[512,128]{1,0:T(8,128)}, f32[512,128]{1,0:T(8,128)}) custom-call(s32[20,128]{1,0:T(8,128)} %get-tuple-element.16.lim_ref, bf16[2048,128]{1,0:T(8,128)(2,1)} %bitcast.27, bf16[2048,128]{1,0:T(8,128)(2,1)} %bitcast.30, bf16[512,128]{1,0:T(8,128)(2,1)} %bitcast.19, bf16[512,128]{1,0:T(8,128)(2,1)} %bitcast.22, ...), custom_call_target="tpu_custom_call" | custom-call | flops 2000000000 | bytes 1000000 | tf_op jit(solution)/shard_map/own_grads/pallas_call | solution.py:305
  42.8 0.4 collective-permute-start.6
  43.2 1.4 %collective-permute-start.10 = (bf16[256,128]{1,0:T(8,128)(2,1)S(1)}, bf16[256,128]{1,0:T(8,128)(2,1)S(1)}, u32[]{:S(2)}, u32[]{:S(2)}) collective-permute-start(bf16[256,128]{1,0:T(8,128)(2,1)S(1)} %get-tuple-element.34), channel_id=1, source_target_pairs={{0,4},{4,8},{8,12},{12,0},{1,5},{5,9},{9,13},{13,1},{2,6},{6,10},{... | collective-permute-start | bytes 196616 | tf_op jit(solution)/shard_map/ppermute | solution.py:300
  44.6 2.5 %collective-permute-start.8 = (bf16[256,128]{1,0:T(8,128)(2,1)S(1)}, bf16[256,128]{1,0:T(8,128)(2,1)S(1)}, u32[]{:S(2)}, u32[]{:S(2)}) collective-permute-start(bf16[256,128]{1,0:T(8,128)(2,1)S(1)} %get-tuple-element.36), channel_id=1, source_target_pairs={{0,12},{4,0},{8,4},{12,8},{1,13},{5,1},{9,5},{13,9},{2,14},{6,2},{... | collective-permute-start | bytes 196616 | tf_op jit(solution)/shard_map/ppermute | solution.py:300
  47.1 0.0 collective-permute-start.9
  47.1 0.0 collective-permute-done.6.recv_ref
  47.1 2.7 %collective-permute-done.10.refs_2_ = bf16[256,128]{1,0:T(8,128)(2,1)S(1)} collective-permute-done((bf16[256,128]{1,0:T(8,128)(2,1)S(1)}, bf16[256,128]{1,0:T(8,128)(2,1)S(1)}, u32[]{:S(2)}, u32[]{:S(2)}) %collective-permute-start.10) | collective-permute-done | bytes 65568 | tf_op jit(solution)/shard_map/ppermute | solution.py:300
  49.8 0.4 collective-permute-done.8.refs_0_
  50.2 3.1 %collective-permute-done.9.refs_1_ = bf16[256,128]{1,0:T(8,128)(2,1)S(1)} collective-permute-done((bf16[256,128]{1,0:T(8,128)(2,1)S(1)}, bf16[256,128]{1,0:T(8,128)(2,1)S(1)}, u32[]{:S(2)}, u32[]{:S(2)}) %collective-permute-start.9) | collective-permute-done | bytes 65568 | tf_op jit(solution)/shard_map/ppermute | solution.py:300
  53.3 0.6 %copy-done.4 = bf16[256,128]{1,0:T(8,128)(2,1)} copy-done((bf16[256,128]{1,0:T(8,128)(2,1)}, bf16[256,128]{1,0:T(8,128)(2,1)S(1)}, u32[]{:S(2)}) %copy-start.4) | copy-done | bytes 65560
  53.9 1.8 %combine.1 = bf16[512,128]{1,0:T(8,128)(2,1)} custom-call(s32[3,128]{1,0:T(4,128)} %get-tuple-element.24.send_ref, f32[512,128]{1,0:T(8,128)} %get-tuple-element.25.keep_ref, f32[512,128]{1,0:T(8,128)} %copy-done.1, bf16[256,128]{1,0:T(8,128)(2,1)} %copy-done.3, bf16[256,128]{1,0:T(8,128)(2,1)} %copy-done.4, bf16[256,128]{1,0:T(8,128)(2,1)} %copy-done.2), custom_call_target="tpu_custom_call" | custom-call | tf_op jit(solution)/shard_map/combine/pallas_call | solution.py:331
  55.7 1.6 %collective-permute-done.11 = bf16[512,128]{1,0:T(8,128)(2,1)S(1)} collective-permute-done((bf16[512,128]{1,0:T(8,128)(2,1)}, bf16[512,128]{1,0:T(8,128)(2,1)S(1)}, u32[]{:S(2)}, u32[]{:S(2)}) %collective-permute-start.11) | collective-permute-done | bytes 131104 | tf_op jit(solution)/shard_map/ppermute | solution.py:339
  57.3 1.6 %select_bitcast_fusion = (bf16[512,1,128]{2,0,1:T(8,128)(2,1)}, bf16[512,1,128]{2,0,1:T(8,128)(2,1)}) fusion(bf16[512,128]{1,0:T(8,128)(2,1)S(1)} %collective-permute-done.11, bf16[512,128]{1,0:T(8,128)(2,1)} %combine.1, pred[]{:T(512)S(6)} %eq.4), kind=kLoop, calls=%fused_computation.1 | loop fusion | flops 131072 | bytes 524289 | tf_op jit(solution)/shard_map/reshape | solution.py:341
  (22 shorter events, 0.1 us)
Async XLA Ops:
  2.7 7.7 %collective-permute-start = (bf16[256,128]{1,0:T(8,128)(2,1)}, bf16[256,128]{1,0:T(8,128)(2,1)S(1)}, u32[]{:S(2)}, u32[]{:S(2)}) collective-permute-start(bf16[256,128]{1,0:T(8,128)(2,1)} %get-tuple-element.17), channel_id=1, source_target_pairs={{0,4},{4,8},{8,12},{12,0},{1,5},{5,9},{9,13},{13,1},{2,6},{6,10},{... | collective-permute-start | bytes 196616 | tf_op jit(solution)/shard_map/ppermute | solution.py:253
  5.7 7.3 %collective-permute-start.1 = (bf16[256,128]{1,0:T(8,128)(2,1)}, bf16[256,128]{1,0:T(8,128)(2,1)S(1)}, u32[]{:S(2)}, u32[]{:S(2)}) collective-permute-start(bf16[256,128]{1,0:T(8,128)(2,1)} %get-tuple-element.18), channel_id=1, source_target_pairs={{0,8},{4,12},{8,0},{12,4},{1,9},{5,13},{9,1},{13,5},{2,10},{6,14},... | collective-permute-start | bytes 196616 | tf_op jit(solution)/shard_map/ppermute | solution.py:253
  8.3 4.9 %collective-permute-start.2 = (bf16[256,128]{1,0:T(8,128)(2,1)}, bf16[256,128]{1,0:T(8,128)(2,1)S(1)}, u32[]{:S(2)}, u32[]{:S(2)}) collective-permute-start(bf16[256,128]{1,0:T(8,128)(2,1)} %get-tuple-element.19), channel_id=1, source_target_pairs={{0,12},{4,0},{8,4},{12,8},{1,13},{5,1},{9,5},{13,9},{2,14},{6,2},{... | collective-permute-start | bytes 196616 | tf_op jit(solution)/shard_map/ppermute | solution.py:253
  10.4 9.9 %copy-start.5 = (bf16[256,128]{1,0:T(8,128)(2,1)}, bf16[256,128]{1,0:T(8,128)(2,1)S(1)}, u32[]{:S(2)}) copy-start(bf16[256,128]{1,0:T(8,128)(2,1)S(1)} %collective-permute-done.refs_0_) | copy-start | bytes 196612
  10.4 9.9 %collective-permute-start.3 = (bf16[256,128]{1,0:T(8,128)(2,1)S(1)}, bf16[256,128]{1,0:T(8,128)(2,1)S(1)}, u32[]{:S(2)}, u32[]{:S(2)}) collective-permute-start(bf16[256,128]{1,0:T(8,128)(2,1)S(1)} %collective-permute-done.refs_0_), channel_id=1, source_target_pairs={{0,1},{1,0},{2,3},{3,2},{4,5},{5,4},{6,7},{7,6},{8,9},{9,8},{10,11... | collective-permute-start | bytes 196616 | tf_op jit(solution)/shard_map/ppermute | solution.py:268
  13.0 7.3 %copy-start.6 = (bf16[256,128]{1,0:T(8,128)(2,1)}, bf16[256,128]{1,0:T(8,128)(2,1)S(1)}, u32[]{:S(2)}) copy-start(bf16[256,128]{1,0:T(8,128)(2,1)S(1)} %collective-permute-done.1.refs_1_) | copy-start | bytes 196612
  13.0 7.3 %collective-permute-start.4 = (bf16[256,128]{1,0:T(8,128)(2,1)S(1)}, bf16[256,128]{1,0:T(8,128)(2,1)S(1)}, u32[]{:S(2)}, u32[]{:S(2)}) collective-permute-start(bf16[256,128]{1,0:T(8,128)(2,1)S(1)} %collective-permute-done.1.refs_1_), channel_id=1, source_target_pairs={{0,1},{1,0},{2,3},{3,2},{4,5},{5,4},{6,7},{7,6},{8,9},{9,8},{10,11... | collective-permute-start | bytes 196616 | tf_op jit(solution)/shard_map/ppermute | solution.py:268
  13.2 7.1 %copy-start.7 = (bf16[256,128]{1,0:T(8,128)(2,1)}, bf16[256,128]{1,0:T(8,128)(2,1)S(1)}, u32[]{:S(2)}) copy-start(bf16[256,128]{1,0:T(8,128)(2,1)S(1)} %collective-permute-done.2.refs_2_) | copy-start | bytes 196612
  13.2 7.1 %collective-permute-start.5 = (bf16[256,128]{1,0:T(8,128)(2,1)S(1)}, bf16[256,128]{1,0:T(8,128)(2,1)S(1)}, u32[]{:S(2)}, u32[]{:S(2)}) collective-permute-start(bf16[256,128]{1,0:T(8,128)(2,1)S(1)} %collective-permute-done.2.refs_2_), channel_id=1, source_target_pairs={{0,1},{1,0},{2,3},{3,2},{4,5},{5,4},{6,7},{7,6},{8,9},{9,8},{10,11... | collective-permute-start | bytes 196616 | tf_op jit(solution)/shard_map/ppermute | solution.py:268
  20.3 0.6 %copy-start.8 = (bf16[256,128]{1,0:T(8,128)(2,1)}, bf16[256,128]{1,0:T(8,128)(2,1)S(1)}, u32[]{:S(2)}) copy-start(bf16[256,128]{1,0:T(8,128)(2,1)S(1)} %collective-permute-done.3.refs_3_) | copy-start | bytes 196612
  20.3 0.6 %copy-start.9 = (bf16[256,128]{1,0:T(8,128)(2,1)}, bf16[256,128]{1,0:T(8,128)(2,1)S(1)}, u32[]{:S(2)}) copy-start(bf16[256,128]{1,0:T(8,128)(2,1)S(1)} %collective-permute-done.4.refs_4_) | copy-start | bytes 196612
  20.9 0.6 %copy-start.10 = (bf16[256,128]{1,0:T(8,128)(2,1)}, bf16[256,128]{1,0:T(8,128)(2,1)S(1)}, u32[]{:S(2)}) copy-start(bf16[256,128]{1,0:T(8,128)(2,1)S(1)} %collective-permute-done.5.refs_5_) | copy-start | bytes 196612
  33.0 10.1 %collective-permute-start.7 = (f32[768,128]{1,0:T(8,128)}, f32[768,128]{1,0:T(8,128)S(1)}, u32[]{:S(2)}, u32[]{:S(2)}) collective-permute-start(f32[768,128]{1,0:T(8,128)} %get-tuple-element.28), channel_id=1, source_target_pairs={{0,1},{1,0},{2,3},{3,2},{4,5},{5,4},{6,7},{7,6},{8,9},{9,8},{10,11... | collective-permute-start | bytes 1179656 | tf_op jit(solution)/shard_map/ppermute | solution.py:297
  33.3 9.8 %copy-start = (f32[768,128]{1,0:T(8,128)S(1)}, f32[768,128]{1,0:T(8,128)}, u32[]{:S(2)}) copy-start(f32[768,128]{1,0:T(8,128)} %get-tuple-element.27) | copy-start | bytes 1179652
  42.8 4.3 %collective-permute-start.6 = (f32[512,128]{1,0:T(8,128)}, f32[512,128]{1,0:T(8,128)S(1)}, u32[]{:S(2)}, u32[]{:S(2)}) collective-permute-start(f32[512,128]{1,0:T(8,128)} %get-tuple-element.26), channel_id=1, source_target_pairs={{0,1},{1,0},{2,3},{3,2},{4,5},{5,4},{6,7},{7,6},{8,9},{9,8},{10,11... | collective-permute-start | bytes 786440 | tf_op jit(solution)/shard_map/ppermute | solution.py:330
  43.2 6.6 %collective-permute-start.10 = (bf16[256,128]{1,0:T(8,128)(2,1)S(1)}, bf16[256,128]{1,0:T(8,128)(2,1)S(1)}, u32[]{:S(2)}, u32[]{:S(2)}) collective-permute-start(bf16[256,128]{1,0:T(8,128)(2,1)S(1)} %get-tuple-element.34), channel_id=1, source_target_pairs={{0,4},{4,8},{8,12},{12,0},{1,5},{5,9},{9,13},{13,1},{2,6},{6,10},{... | collective-permute-start | bytes 196616 | tf_op jit(solution)/shard_map/ppermute | solution.py:300
  44.6 5.6 %collective-permute-start.8 = (bf16[256,128]{1,0:T(8,128)(2,1)S(1)}, bf16[256,128]{1,0:T(8,128)(2,1)S(1)}, u32[]{:S(2)}, u32[]{:S(2)}) collective-permute-start(bf16[256,128]{1,0:T(8,128)(2,1)S(1)} %get-tuple-element.36), channel_id=1, source_target_pairs={{0,12},{4,0},{8,4},{12,8},{1,13},{5,1},{9,5},{13,9},{2,14},{6,2},{... | collective-permute-start | bytes 196616 | tf_op jit(solution)/shard_map/ppermute | solution.py:300
  47.1 6.2 %collective-permute-start.9 = (bf16[256,128]{1,0:T(8,128)(2,1)S(1)}, bf16[256,128]{1,0:T(8,128)(2,1)S(1)}, u32[]{:S(2)}, u32[]{:S(2)}) collective-permute-start(bf16[256,128]{1,0:T(8,128)(2,1)S(1)} %get-tuple-element.35), channel_id=1, source_target_pairs={{0,8},{4,12},{8,0},{12,4},{1,9},{5,13},{9,1},{13,5},{2,10},{6,14},... | collective-permute-start | bytes 196616 | tf_op jit(solution)/shard_map/ppermute | solution.py:300
  47.1 6.2 %copy-start.1 = (f32[512,128]{1,0:T(8,128)}, f32[512,128]{1,0:T(8,128)S(1)}, u32[]{:S(2)}) copy-start(f32[512,128]{1,0:T(8,128)S(1)} %collective-permute-done.6.recv_ref) | copy-start | bytes 786436
  49.8 3.5 %copy-start.2 = (bf16[256,128]{1,0:T(8,128)(2,1)}, bf16[256,128]{1,0:T(8,128)(2,1)S(1)}, u32[]{:S(2)}) copy-start(bf16[256,128]{1,0:T(8,128)(2,1)S(1)} %collective-permute-done.10.refs_2_) | copy-start | bytes 196612
  50.2 3.1 %copy-start.3 = (bf16[256,128]{1,0:T(8,128)(2,1)}, bf16[256,128]{1,0:T(8,128)(2,1)S(1)}, u32[]{:S(2)}) copy-start(bf16[256,128]{1,0:T(8,128)(2,1)S(1)} %collective-permute-done.8.refs_0_) | copy-start | bytes 196612
  53.3 0.6 %copy-start.4 = (bf16[256,128]{1,0:T(8,128)(2,1)}, bf16[256,128]{1,0:T(8,128)(2,1)S(1)}, u32[]{:S(2)}) copy-start(bf16[256,128]{1,0:T(8,128)(2,1)S(1)} %collective-permute-done.9.refs_1_) | copy-start | bytes 196612
  55.7 1.6 %collective-permute-start.11 = (bf16[512,128]{1,0:T(8,128)(2,1)}, bf16[512,128]{1,0:T(8,128)(2,1)S(1)}, u32[]{:S(2)}, u32[]{:S(2)}) collective-permute-start(bf16[512,128]{1,0:T(8,128)(2,1)} %combine.1), channel_id=1, source_target_pairs={{0,1},{1,0},{2,3},{3,2},{4,5},{5,4},{6,7},{7,6},{8,9},{9,8},{10,11... | collective-permute-start | bytes 393224 | tf_op jit(solution)/shard_map/ppermute | solution.py:339
